TPU v7x, 32 devices: a whole 2x2x4 slice. The times are simulated.
32 devices in a mesh: dp: 8 (over y, x, core), mp: 4 (over z).
Axes of the slice: x: 2, y: 2, z: 4, core: 2. Of those that a mesh axis runs over, the one named last changes fastest.
Arguments:
- candidates: bfloat16 [64, 256, 768], P('dp', 'mp'), may hold values from -6 to 6
- owner_row: int32 [64], replicated, may hold values from 0 to 63, as said below
- selected: int32 [16], replicated, may hold values from 0 to 63, as said below
- dest_slot: int32 [16], replicated, may hold values from 0 to 15, as said below
- patch_weight: bfloat16 [768, 768], P(None, 'mp'), may hold values from -0.21875 to 0.21875
- positions: bfloat16 [256, 768], P(None, 'mp'), may hold values from -3 to 3
- qkv_weight: bfloat16 [768, 3, 768], P(None, None, 'mp'), may hold values from -1 to 1
- out_weight: bfloat16 [768, 768], P('mp'), may hold values from -0.21875 to 0.21875
- attn_gain: bfloat16 [768], replicated, may hold values from 0.099609375 to 1.8984375
- mlp_gain: bfloat16 [768], replicated, may hold values from 0.099609375 to 1.8984375
- up_weight: bfloat16 [768, 3072], P(None, 'mp'), may hold values from -0.21875 to 0.21875
- down_weight: bfloat16 [3072, 768], P('mp'), may hold values from -0.109375 to 0.109375
Outputs:
- layer_out: bfloat16 [16, 256, 768], P('dp', 'mp')
Inputs may be any that keep to these rules, and one draw needn't show every extreme that they name: `owner_row`: a permutation; storage row r sits on index r // 8 of dp. `selected`: distinct candidates; no index of dp stores more than 4 of them, and some index stores exactly 4. `dest_slot`: a permutation; the 2 slots s with equal s // 2 get candidates stored on different indices of dp.
All inputs are finite; a program needn't handle non-finite values.
Results may differ from a plain program's by a relative error of at most 0.012.
Values may be sent and summed in bfloat16 or wider, within the bound.
No kernel may reach another device: no remote copies, remote signals or barrier semaphores. Data moves between devices by JAX's collectives and lax.ppermute only.
A program may use at most 128 MiB of HBM per device.

v0:
```python
import jax
import jax.numpy as jnp
from jax import lax
from jax.sharding import PartitionSpec as P

PATCHES = 256
CAND_DEV = 8
SEL_DEV = 2
HEAD_DIM = 64


def norm_rows(values, gain):
    average = jnp.mean(values, axis=-1, keepdims=True)
    centred = values - average
    variance = jnp.mean(centred * centred, axis=-1, keepdims=True)
    return centred * lax.rsqrt(variance + 1e-06) * gain.astype(jnp.float32)


def local(
    candidates,
    owner_row,
    selected,
    dest_slot,
    patch_weight,
    positions,
    qkv_weight,
    out_weight,
    attn_gain,
    mlp_gain,
    up_weight,
    down_weight,
):
    learners = lax.axis_size("dp")
    own_index = lax.axis_index("dp")
    quarter = candidates.shape[1]
    pixel_width = candidates.shape[2]
    chosen_rows = jnp.take(owner_row, selected)
    slot_rows = jnp.zeros(dest_slot.shape, jnp.int32).at[dest_slot].set(chosen_rows)
    source_owner = slot_rows // CAND_DEV
    local_row = slot_rows % CAND_DEV
    stored = candidates.reshape(CAND_DEV, quarter * pixel_width)
    mine = (source_owner == own_index).reshape(learners, SEL_DEV)
    picked = jnp.sum(jnp.where(mine, local_row.reshape(learners, SEL_DEV), 0), axis=1)
    outgoing = jnp.take(stored, picked, axis=0)
    incoming = lax.all_to_all(outgoing, "dp", split_axis=0, concat_axis=0, tiled=True)
    senders = lax.dynamic_slice_in_dim(source_owner, own_index * SEL_DEV, SEL_DEV)
    arrived = jnp.take(incoming, senders, axis=0)
    own_pixels = arrived.reshape(SEL_DEV, quarter, pixel_width)
    product = jnp.einsum(
        "brp,pe->bre",
        lax.all_gather(own_pixels, "mp", axis=1, tiled=True),
        patch_weight,
        preferred_element_type=jnp.float32,
    )
    embedded = (product + positions.astype(jnp.float32)[None]).astype(jnp.bfloat16)
    activations = lax.all_gather(embedded, "mp", axis=2, tiled=True).astype(jnp.float32)
    normed = norm_rows(activations, attn_gain).astype(jnp.bfloat16)
    projected = jnp.einsum(
        "btd,dce->btce", normed, qkv_weight, preferred_element_type=jnp.float32
    ).astype(jnp.bfloat16)
    local_heads = qkv_weight.shape[2] // HEAD_DIM
    head_split = projected.reshape(SEL_DEV, PATCHES, 3, local_heads, HEAD_DIM)
    queries = head_split[:, :, 0]
    attn_keys = head_split[:, :, 1]
    attn_values = head_split[:, :, 2]
    scores = jnp.einsum(
        "bqhd,bkhd->bhqk", queries, attn_keys, preferred_element_type=jnp.float32
    ) * HEAD_DIM ** (-0.5)
    attn_probs = jax.nn.softmax(scores, axis=-1).astype(jnp.bfloat16)
    context = jnp.einsum(
        "bhqk,bkhd->bqhd", attn_probs, attn_values, preferred_element_type=jnp.float32
    ).astype(jnp.bfloat16)
    context = context.reshape(SEL_DEV, PATCHES, local_heads * HEAD_DIM)
    partial_out = jnp.einsum("bte,ed->btd", context, out_weight, preferred_element_type=jnp.float32)
    attended = lax.psum(partial_out.astype(jnp.bfloat16), "mp").astype(jnp.float32)
    after_attn = activations + attended
    normed2 = norm_rows(after_attn, mlp_gain).astype(jnp.bfloat16)
    hidden = jax.nn.gelu(
        jnp.einsum("btd,df->btf", normed2, up_weight, preferred_element_type=jnp.float32),
        approximate=False,
    ).astype(jnp.bfloat16)
    down_terms = jnp.einsum("btf,fd->btd", hidden, down_weight, preferred_element_type=jnp.float32)
    summed = lax.psum_scatter(
        down_terms.astype(jnp.bfloat16), "mp", scatter_dimension=1, tiled=True
    ).astype(jnp.float32)
    residual = lax.dynamic_slice_in_dim(after_attn, lax.axis_index("mp") * quarter, quarter, 1)
    return (residual + summed).astype(jnp.bfloat16)


def solution(mesh):
    return jax.shard_map(
        local,
        mesh=mesh,
        in_specs=(
            P("dp", "mp", None),
            P(),
            P(),
            P(),
            P(None, "mp"),
            P(None, "mp"),
            P(None, None, "mp"),
            P("mp", None),
            P(),
            P(),
            P(None, "mp"),
            P("mp", None),
        ),
        out_specs=P("dp", "mp", None),
        check_vma=False,
    )
```

profile of v0, /device:TPU:0, one launch (start us, length us, event | category | flops | bytes accessed | tf_op | source)
XLA Modules:
  0.0 183.8 jit_solution(13271876456663978697)
XLA Ops:
  6.5 0.8 compare_select_fusion.3
  7.3 1.3 gather_fusion
  10.2 1.6 copy.77
  11.8 1.1 gather_fusion.1
  13.5 1.2 reduce.4
  14.7 1.5 reshape.149
  16.2 5.2 %all-to-all-start = ((bf16[8,2,24576]{2,1,0:T(2,128)(2,1)}), bf16[8,2,24576]{2,1,0:T(2,128)(2,1)S(1)}, u32[]{:S(2)}, u32[]{:S(2)}) async-start(bf16[8,2,24576]{2,1,0:T(2,128)(2,1)} %reshape.149), calls=%async_computation | async-start | bytes 1572864 | tf_op jit(solution)/shard_map/all_to_all | solution.py:45
  22.3 11.7 %all-to-all-done = bf16[8,2,24576]{2,1,0:T(2,128)(2,1)S(1)} async-done(((bf16[8,2,24576]{2,1,0:T(2,128)(2,1)}), bf16[8,2,24576]{2,1,0:T(2,128)(2,1)S(1)}, u32[]{:S(2)}, u32[]{:S(2)}) %all-to-all-start) | async-done | bytes 786464 | tf_op jit(solution)/shard_map/all_to_all | solution.py:45
  34.0 0.8 reshape.150
  34.8 0.9 copy.82
  35.7 0.8 gather_fusion.2
  36.6 18.1 %all_gather.6 = bf16[2,256,768]{2,1,0:T(8,128)(2,1)S(1)} all-gather(bf16[2,64,768]{2,1,0:T(8,128)(2,1)S(1)} %bitcast_select_fusion.1), channel_id=1, replica_groups=mesh['dp'=8,'mp'=4] {'mp'}, dimensions={1}, use_global_device_ids=true | all-gather | bytes 983040 | tf_op jit(solution)/shard_map/all_gather | solution.py:51
  55.3 17.4 %all_gather.7 = bf16[2,256,768]{1,0,2:T(2,128)(2,1)S(1)} all-gather(bf16[2,256,192]{1,0,2:T(2,128)(2,1)S(1)} %copy.63), channel_id=1, replica_groups=mesh['dp'=8,'mp'=4] {'mp'}, dimensions={2}, use_global_device_ids=true | all-gather | bytes 983040 | tf_op jit(solution)/shard_map/all_gather | solution.py:56
  74.5 0.8 convolution_convert_fusion.2
  76.0 0.9 convolution_convert_fusion.3
  76.9 1.3 convolution_convert_fusion.1
  78.5 44.0 %all-reduce.4.cloned.1.call-done = bf16[2,256,768]{2,1,0:T(8,128)(2,1)} async-done(((bf16[2,256,768]{2,1,0:T(8,128)(2,1)}), bf16[2,256,768]{2,1,0:T(8,128)(2,1)}) %all-reduce.4.cloned.1.call-update) | async-done | bytes 786448 | tf_op jit(solution)/shard_map/psum | solution.py:75
  122.5 1.5 fusion.107
  124.5 1.3 fusion.63
  125.7 4.4 %convolution_convert_fusion = bf16[2,256,768]{2,1,0:T(8,128)(2,1)S(1)} fusion(bf16[768,768]{1,0:T(8,128)(2,1)S(1)} %copy-done.8, f32[2,256,768]{2,1,0:T(8,128)S(1)} %get-tuple-element.13, u8[256,768]{1,0:T(8,128)(4,1)S(1)} %get-tuple-element.6, u8[256,768]{1,0:T(8,128)(4,1)S(1)} %get-tuple-element.5), kind=kOutput, calls=%fused_computation.41 | convolution fusion | flops 631898112 | bytes 3932160 | tf_op jit(solution)/shard_map/btf,fd->btd/dot_general | solution.py:82
  130.2 1.7 copy.69
  133.2 42.0 %all-reduce.6.cloned.1.call-done = bf16[2,256,768]{2,0,1:T(2,128)(2,1)} async-done(((bf16[2,256,768]{2,0,1:T(2,128)(2,1)}), bf16[2,256,768]{2,0,1:T(2,128)(2,1)}) %all-reduce.6.cloned.1.call-update) | async-done | bytes 786448
  175.2 1.1 constant_dynamic-slice_fusion
  176.3 0.7 add_convert_fusion
  (55 shorter events, 7.5 us)
Async XLA Ops:
  6.5 117.9 %copy-start = (bf16[768,768]{1,0:T(8,128)(2,1)S(1)}, bf16[768,768]{1,0:T(8,128)(2,1)}, u32[]{:S(2)}) copy-start(bf16[768,768]{1,0:T(8,128)(2,1)} %param.22) | copy-start | bytes 3538948
  14.7 6.8 %copy-start.5 = (bf16[256,192]{0,1:T(8,128)(2,1)S(1)}, bf16[256,192]{0,1:T(8,128)(2,1)}, u32[]{:S(2)}) copy-start(bf16[256,192]{0,1:T(8,128)(2,1)} %param.17) | copy-start | bytes 294916
  14.7 7.5 %copy-start.6 = (bf16[768]{0:T(1024)(128)(2,1)S(1)}, bf16[768]{0:T(1024)(128)(2,1)}, u32[]{:S(2)}) copy-start(bf16[768]{0:T(1024)(128)(2,1)} %param.20) | copy-start | bytes 4612
  16.2 17.8 %all-to-all-start = ((bf16[8,2,24576]{2,1,0:T(2,128)(2,1)}), bf16[8,2,24576]{2,1,0:T(2,128)(2,1)S(1)}, u32[]{:S(2)}, u32[]{:S(2)}) async-start(bf16[8,2,24576]{2,1,0:T(2,128)(2,1)} %reshape.149), calls=%async_computation | async-start | bytes 1572864 | tf_op jit(solution)/shard_map/all_to_all | solution.py:45
  21.4 101.1 %all-reduce.4.cloned.1.call-start = ((), (), s32[]{:S(2)}) async-start(), calls=%async_computation.1 | async-start | bytes 1572864 | tf_op jit(solution)/shard_map/psum | solution.py:75
  35.7 19.0 %copy-start.2 = (f32[256,192]{0,1:T(8,128)S(1)}, f32[256,192]{0,1:T(8,128)}, u32[]{:S(2)}) copy-start(f32[256,192]{0,1:T(8,128)} %convert_element_type.51) | copy-start | bytes 589828
  35.7 19.0 %copy-start.4 = (bf16[768,192]{0,1:T(8,128)(2,1)S(1)}, bf16[768,192]{0,1:T(8,128)(2,1)}, u32[]{:S(2)}) copy-start(bf16[768,192]{0,1:T(8,128)(2,1)} %param.16) | copy-start | bytes 884740
  73.3 1.2 copy-start.9
  76.0 1.0 copy-start.3
  76.9 1.6 copy-start.7
  78.3 96.9 %all-reduce.6.cloned.1.call-start = ((), (), s32[]{:S(2)}) async-start(), calls=%async_computation.2 | async-start | bytes 1572864
  122.5 1.5 copy-start.1
  124.4 1.3 copy-start.8
  130.2 1.8 copy-start.10
Sparse Core Ops, SparseCore 0:
  78.4 44.0 all-reduce.3
  132.0 43.1 all-reduce.5
where the time goes:
time: 184 us
  waiting for transfers between devices  97.8 us (53%)
  blocking collectives  35.5 us (19%)
  between operations  14.3 us (8%)
  local copies, waits for them, and re-layouts  14 us (8%)
  matrix products  9.79 us (5%)
  other arithmetic  7.02 us (4%)
  starting transfers between devices  5.46 us (3%)
    psum x1, waiting for transfers between devices, local(): lax.psum(partial_out.astype(jnp.bfloat16), 'mp').astype(jnp.float32)  44 us
    unnamed x3, waiting for transfers between devices  42.1 us
    all_gather x1, blocking collectives, local(): lax.all_gather(own_pixels, 'mp', axis=1, tiled=True)  18.1 us
    all_gather x1, blocking collectives, local(): lax.all_gather(embedded, 'mp', axis=2, tiled=True).astype(jnp.float32)  17.4 us
    all_to_all x1, waiting for transfers between devices, local(): lax.all_to_all(outgoing, 'dp', split_axis=0, concat_axis=0, tiled=True)  11.7 us
    unnamed x28, local copies, waits for them, and re-layouts  7.11 us
    all_to_all x1, starting transfers between devices, local(): lax.all_to_all(outgoing, 'dp', split_axis=0, concat_axis=0, tiled=True)  5.2 us
    dot_general x1, matrix products, local(): jnp.einsum('btf,fd->btd', hidden, down_weight, preferred_element_type=jnp...  4.43 us
  transfers between devices with their start and end apart: 3, of which 3 were waited for; matrix products, arithmetic and copies ran while one was open for 1% of the time, Pallas kernels for 0%

commit v1 on v0

--- a/solution.py
+++ b/solution.py
@@ -72,7 +72,9 @@
     ).astype(jnp.bfloat16)
     context = context.reshape(SEL_DEV, PATCHES, local_heads * HEAD_DIM)
     partial_out = jnp.einsum("bte,ed->btd", context, out_weight, preferred_element_type=jnp.float32)
-    attended = lax.psum(partial_out.astype(jnp.bfloat16), "mp").astype(jnp.float32)
+    attended = jnp.sum(lax.all_gather(partial_out.astype(jnp.bfloat16), "mp"), axis=0).astype(
+        jnp.float32
+    )
     after_attn = activations + attended
     normed2 = norm_rows(after_attn, mlp_gain).astype(jnp.bfloat16)
     hidden = jax.nn.gelu(

time: 184 us -> 207 us (1.12)
  waiting for transfers between devices: 97.8 us -> 117 us
  other arithmetic: 7.02 us -> 10.5 us
    all_gather x0 -> x1, waiting for transfers between devices: none -> 63.5 us  [local(): lax.all_gather(partial_out.astype(jnp.bfloat16), 'mp')]
    psum x1 -> x0, waiting for transfers between devices: 44 us -> none  [local(): lax.psum(partial_out.astype(jnp.bfloat16), 'mp').astype(jnp.float32)]
    reduce_sum x0 -> x1, other arithmetic: none -> 2.6 us  [local(): jnp.sum(lax.all_gather(partial_out.astype(jnp.bfloat16), 'mp'), axis=0)]
    unnamed x28 -> x26, local copies, waits for them, and re-layouts: 7.11 us -> 7.12 us
where the time goes in v1:
time: 207 us; the launch traced here: 206 us
  waiting for transfers between devices  117 us (57%)
  blocking collectives  35.5 us (17%)
  between operations  14.3 us (7%)
  local copies, waits for them, and re-layouts  14 us (7%)
  other arithmetic  10.5 us (5%)
  matrix products  9.72 us (5%)
  starting transfers between devices  5.46 us (3%)
    all_gather x1, waiting for transfers between devices, local(): lax.all_gather(partial_out.astype(jnp.bfloat16), 'mp')  63.5 us
    unnamed x3, waiting for transfers between devices  41.4 us
    all_gather x1, blocking collectives, local(): lax.all_gather(own_pixels, 'mp', axis=1, tiled=True)  18.1 us
    all_gather x1, blocking collectives, local(): lax.all_gather(embedded, 'mp', axis=2, tiled=True).astype(jnp.float32)  17.4 us
    all_to_all x1, waiting for transfers between devices, local(): lax.all_to_all(outgoing, 'dp', split_axis=0, concat_axis=0, tiled=True)  11.7 us
    unnamed x26, local copies, waits for them, and re-layouts  7.12 us
    all_to_all x1, starting transfers between devices, local(): lax.all_to_all(outgoing, 'dp', split_axis=0, concat_axis=0, tiled=True)  5.2 us
    dot_general x1, matrix products, local(): jnp.einsum('btf,fd->btd', hidden, down_weight, preferred_element_type=jnp...  4.41 us
  transfers between devices with their start and end apart: 3, of which 3 were waited for; matrix products, arithmetic and copies ran while one was open for 1% of the time, Pallas kernels for 0%

profile of v1, /device:TPU:0, one launch (start us, length us, event | category | flops | bytes accessed | tf_op | source)
XLA Modules:
  0.0 206.1 jit_solution(14278742000363332639)
XLA Ops:
  7.3 1.3 gather_fusion
  10.2 1.6 copy.75
  11.8 1.1 gather_fusion.1
  13.5 1.2 reduce.5
  14.7 1.5 reshape.150
  16.2 5.2 %all-to-all-start = ((bf16[8,2,24576]{2,1,0:T(2,128)(2,1)}), bf16[8,2,24576]{2,1,0:T(2,128)(2,1)S(1)}, u32[]{:S(2)}, u32[]{:S(2)}) async-start(bf16[8,2,24576]{2,1,0:T(2,128)(2,1)} %reshape.150), calls=%async_computation | async-start | bytes 1572864 | tf_op jit(solution)/shard_map/all_to_all | solution.py:45
  22.3 11.7 %all-to-all-done = bf16[8,2,24576]{2,1,0:T(2,128)(2,1)S(1)} async-done(((bf16[8,2,24576]{2,1,0:T(2,128)(2,1)}), bf16[8,2,24576]{2,1,0:T(2,128)(2,1)S(1)}, u32[]{:S(2)}, u32[]{:S(2)}) %all-to-all-start) | async-done | bytes 786464 | tf_op jit(solution)/shard_map/all_to_all | solution.py:45
  34.0 0.8 reshape.151
  34.8 0.9 copy.80
  35.7 0.8 gather_fusion.2
  36.6 18.1 %all_gather.12 = bf16[2,256,768]{2,1,0:T(8,128)(2,1)S(1)} all-gather(bf16[2,64,768]{2,1,0:T(8,128)(2,1)S(1)} %bitcast_select_fusion.1), channel_id=1, replica_groups=mesh['dp'=8,'mp'=4] {'mp'}, dimensions={1}, use_global_device_ids=true | all-gather | bytes 983040 | tf_op jit(solution)/shard_map/all_gather | solution.py:51
  55.3 17.4 %all_gather.13 = bf16[2,256,768]{1,0,2:T(2,128)(2,1)S(1)} all-gather(bf16[2,256,192]{1,0,2:T(2,128)(2,1)S(1)} %copy.61), channel_id=1, replica_groups=mesh['dp'=8,'mp'=4] {'mp'}, dimensions={2}, use_global_device_ids=true | all-gather | bytes 983040 | tf_op jit(solution)/shard_map/all_gather | solution.py:56
  74.5 0.8 convolution_convert_fusion.2
  76.0 0.9 convolution_convert_fusion.3
  76.9 1.3 convolution_convert_fusion.1
  78.5 63.5 %all-gather.3.cloned.1.call-done = bf16[8,256,768]{2,1,0:T(8,128)(2,1)} async-done(((bf16[2,256,768]{2,1,0:T(8,128)(2,1)}), bf16[8,256,768]{2,1,0:T(8,128)(2,1)}) %all-gather.3.cloned.1.call-update) | async-done | bytes 3145744 | tf_op jit(solution)/shard_map/all_gather | solution.py:75
  142.0 2.6 %reduce_sum.73 = bf16[2,256,768]{2,1,0:T(8,128)(2,1)S(1)} reduce(bf16[4,2,256,768]{3,2,1,0:T(8,128)(2,1)} %bitcast.81, bf16[]{:T(256)} %constant.72.clone.1), dimensions={0}, to_apply=%region_6.7 | reduce | flops 1179648 | bytes 3932162 | tf_op jit(solution)/shard_map/reduce_sum | solution.py:75
  144.9 1.5 multiply_reduce_fusion
  146.4 1.2 fusion.63
  147.7 4.4 %convolution_convert_fusion = bf16[2,256,768]{2,1,0:T(8,128)(2,1)S(1)} fusion(bf16[768,768]{1,0:T(8,128)(2,1)S(1)} %copy-done.7, f32[2,256,768]{2,1,0:T(8,128)S(1)} %get-tuple-element.13, u8[256,768]{1,0:T(8,128)(4,1)S(1)} %get-tuple-element.6, u8[256,768]{1,0:T(8,128)(4,1)S(1)} %get-tuple-element.5), kind=kOutput, calls=%fused_computation.41 | convolution fusion | flops 631898112 | bytes 3932160 | tf_op jit(solution)/shard_map/btf,fd->btd/dot_general | solution.py:84
  152.1 1.7 copy.67
  155.1 41.4 %all-reduce.3.cloned.1.call-done = bf16[2,256,768]{2,0,1:T(2,128)(2,1)} async-done(((bf16[2,256,768]{2,0,1:T(2,128)(2,1)}), bf16[2,256,768]{2,0,1:T(2,128)(2,1)}) %all-reduce.3.cloned.1.call-update) | async-done | bytes 786448
  196.5 1.1 constant_dynamic-slice_fusion
  197.5 1.7 add_convert_fusion
  (54 shorter events, 8.1 us)
Async XLA Ops:
  6.5 139.9 %copy-start = (bf16[768,768]{1,0:T(8,128)(2,1)S(1)}, bf16[768,768]{1,0:T(8,128)(2,1)}, u32[]{:S(2)}) copy-start(bf16[768,768]{1,0:T(8,128)(2,1)} %param.22) | copy-start | bytes 3538948
  14.7 6.8 %copy-start.4 = (bf16[256,192]{0,1:T(8,128)(2,1)S(1)}, bf16[256,192]{0,1:T(8,128)(2,1)}, u32[]{:S(2)}) copy-start(bf16[256,192]{0,1:T(8,128)(2,1)} %param.17) | copy-start | bytes 294916
  14.7 7.5 %copy-start.5 = (bf16[768]{0:T(1024)(128)(2,1)S(1)}, bf16[768]{0:T(1024)(128)(2,1)}, u32[]{:S(2)}) copy-start(bf16[768]{0:T(1024)(128)(2,1)} %param.20) | copy-start | bytes 4612
  16.2 17.8 %all-to-all-start = ((bf16[8,2,24576]{2,1,0:T(2,128)(2,1)}), bf16[8,2,24576]{2,1,0:T(2,128)(2,1)S(1)}, u32[]{:S(2)}, u32[]{:S(2)}) async-start(bf16[8,2,24576]{2,1,0:T(2,128)(2,1)} %reshape.150), calls=%async_computation | async-start | bytes 1572864 | tf_op jit(solution)/shard_map/all_to_all | solution.py:45
  21.4 120.6 %all-gather.3.cloned.1.call-start = ((), (), s32[]{:S(2)}) async-start(), calls=%async_computation.1 | async-start | bytes 3932160 | tf_op jit(solution)/shard_map/all_gather | solution.py:75
  35.7 19.0 %copy-start.1 = (f32[256,192]{0,1:T(8,128)S(1)}, f32[256,192]{0,1:T(8,128)}, u32[]{:S(2)}) copy-start(f32[256,192]{0,1:T(8,128)} %convert_element_type.53) | copy-start | bytes 589828
  35.7 19.0 %copy-start.3 = (bf16[768,192]{0,1:T(8,128)(2,1)S(1)}, bf16[768,192]{0,1:T(8,128)(2,1)}, u32[]{:S(2)}) copy-start(bf16[768,192]{0,1:T(8,128)(2,1)} %param.16) | copy-start | bytes 884740
  73.3 1.2 copy-start.8
  76.0 1.0 copy-start.2
  76.9 1.6 copy-start.6
  78.3 118.2 %all-reduce.3.cloned.1.call-start = ((), (), s32[]{:S(2)}) async-start(), calls=%async_computation.2 | async-start | bytes 1572864
  146.4 1.3 copy-start.7
  152.1 1.8 copy-start.9
Sparse Core Ops, SparseCore 0:
  78.4 63.6 all-gather.2
  154.0 42.4 all-reduce.2
